TPU v7x, 128 devices: a whole 4x4x4 slice. The times are simulated.
128 devices in a mesh: expert: 8 (over y, core), mp: 16 (over z, x).
Axes of the slice: x: 4, y: 4, z: 4, core: 2. Of those that a mesh axis runs over, the one named last changes fastest.
Arguments:
- tokens: bfloat16 [2048, 6144], P(('expert', 'mp')), may hold values from -18 to 18
- norm_gain: bfloat16 [6144], replicated, may hold values from 0.099609375 to 1.8984375
- expert_ids: int32 [2048, 2], P(('expert', 'mp')), may hold values from 0 to 7, as said below
- slot_ids: int32 [2048, 2], P(('expert', 'mp')), may hold values from 0 to 7, as said below
- route_weights: float32 [2048, 2], P(('expert', 'mp')), may hold values from 0.1 to 1
- w_gate: bfloat16 [8, 6144, 8192], P('expert', None, 'mp'), may hold values from -0.078125 to 0.078125
- w_up: bfloat16 [8, 6144, 8192], P('expert', None, 'mp'), may hold values from -0.078125 to 0.078125
- w_down: bfloat16 [8, 8192, 6144], P('expert', 'mp'), may hold values from -0.0625 to 0.0625
Outputs:
- moe_out: bfloat16 [2048, 6144], P(('expert', 'mp'))
Inputs may be any that keep to these rules, and one draw needn't show every extreme that they name: `expert_ids`: each token names two different experts. Among the 16 tokens of one device (aligned blocks of rows) no expert is named more than 8 times, and on every device some expert is named exactly 8 times. `slot_ids`: within the tokens of one device, the entries that name the same expert have different slots; slots that no entry names stay empty.
All inputs are finite; a program needn't handle non-finite values.
Results may differ from a plain program's by a relative error of at most 0.015.
Values may be sent and summed in bfloat16 or wider, within the bound.
A program may use at most 128 MiB of HBM per device.

v0:
```python
import jax
import jax.numpy as jnp
from jax import lax
from jax.sharding import PartitionSpec as P

CAP = 8


def local(tokens, norm_gain, expert_ids, slot_ids, route_weights, w_gate, w_up, w_down):
    tok_rows = tokens.shape[0]
    features = tokens.shape[1]
    experts = w_gate.shape[0] * lax.axis_size("expert")
    values = tokens.astype(jnp.float32)
    mean_square = jnp.mean(values * values, axis=1, keepdims=True)
    normed = (values * lax.rsqrt(mean_square + 1e-05) * norm_gain.astype(jnp.float32)).astype(
        jnp.bfloat16
    )
    target = expert_ids * CAP + slot_ids
    places = lax.broadcasted_iota(jnp.int32, (experts * CAP, tok_rows, 2), 0)
    placing = jnp.any(places == target[None, :, :], axis=2).astype(jnp.bfloat16)
    outgoing = jnp.dot(placing, normed, preferred_element_type=jnp.float32).astype(jnp.bfloat16)
    outgoing = outgoing.reshape(experts, CAP, features)
    gate_local = w_gate[0]
    up_local = w_up[0]
    down_local = w_down[0]
    arrived = lax.all_to_all(outgoing, "expert", split_axis=0, concat_axis=0, tiled=True)
    piece = lax.all_gather(arrived.reshape(experts * CAP, features), "mp", axis=0, tiled=True)
    gate_proj = jnp.dot(piece, gate_local, preferred_element_type=jnp.float32)
    up_proj = jnp.dot(piece, up_local, preferred_element_type=jnp.float32)
    hidden = (jax.nn.silu(gate_proj) * up_proj).astype(jnp.bfloat16)
    piece = hidden
    summed = lax.psum_scatter(
        jnp.dot(piece, down_local, preferred_element_type=jnp.float32).astype(jnp.bfloat16),
        "mp",
        scatter_dimension=0,
        tiled=True,
    )
    results = summed.reshape(experts, CAP, features)
    returned = lax.all_to_all(results, "expert", split_axis=0, concat_axis=0, tiled=True)
    flattened = returned.reshape(experts * CAP, features)
    picked = flattened[target].astype(jnp.float32)
    shares = route_weights / (route_weights[:, 0:1] + route_weights[:, 1:2])
    mixed = jnp.sum(shares[:, :, None] * picked, axis=1)
    return mixed.astype(jnp.bfloat16)


def solution(mesh):
    placed = (
        P(("expert", "mp"), None),
        P(),
        P(("expert", "mp"), None),
        P(("expert", "mp"), None),
        P(("expert", "mp"), None),
        P("expert", None, "mp"),
        P("expert", None, "mp"),
        P("expert", "mp", None),
    )
    return jax.shard_map(
        local, mesh=mesh, in_specs=placed, out_specs=P(("expert", "mp"), None), check_vma=False
    )
```

profile of v0, /device:TPU:1, one launch (start us, length us, event | category | flops | bytes accessed | tf_op | source)
XLA Modules:
  0.0 274.3 jit_solution(11265923259628819744)
XLA Ops:
  6.5 0.7 compare_select_fusion
  7.2 0.1 fusion.14
  7.3 0.7 convert_element_type.26
  8.0 1.1 fusion.8
  9.1 1.3 fusion
  10.5 18.0 %all_to_all.10 = bf16[8,8,6144]{2,1,0:T(8,128)(2,1)} all-to-all(bf16[8,8,6144]{2,1,0:T(8,128)(2,1)S(1)} %fusion), channel_id=1, replica_groups=mesh['expert'=8,'mp'=16] {'expert'}, dimensions={0} | all-to-all | bytes 1572864 | tf_op jit(solution)/shard_map/all_to_all | solution.py:26
  28.5 0.0 all-gather.2.cloned.1.call-update
  28.5 0.0 reduce-scatter.2.cloned.1.call-start
  28.5 90.6 %all-gather.2.cloned.1.call-done = bf16[1024,6144]{1,0:T(8,128)(2,1)} async-done(((bf16[64,6144]{1,0:T(8,128)(2,1)}), bf16[1024,6144]{1,0:T(8,128)(2,1)}) %all-gather.2.cloned.1.call-update) | async-done | bytes 12582928 | tf_op jit(solution)/shard_map/all_gather | solution.py:27
  119.1 11.6 %fusion.2 = f32[1024,512]{1,0:T(8,128)S(1)} fusion(bf16[1024,6144]{1,0:T(8,128)(2,1)} %all-gather.2.cloned.1.call-done, bf16[1,6144,512]{2,1,0:T(8,128)(2,1)} %param.14), kind=kOutput, calls=%fused_computation.5 | convolution fusion | flops 6442450944 | bytes 20971520 | tf_op jit(solution)/shard_map/dot_general | solution.py:29
  130.7 0.0 copy-done.1
  130.7 8.9 %multiply_convert_fusion = bf16[1024,512]{1,0:T(8,128)(2,1)S(1)} fusion(f32[1024,512]{1,0:T(8,128)S(1)} %fusion.2, bf16[1024,6144]{1,0:T(8,128)(2,1)S(1)} %copy-done.1, bf16[1,6144,512]{2,1,0:T(8,128)(2,1)} %param.13), kind=kOutput, calls=%fused_computation.9 | convolution fusion | flops 6445596672 | bytes 22020096 | tf_op jit(solution)/shard_map/dot_general | solution.py:28
  139.7 12.4 %convolution_convert_fusion = bf16[1024,6144]{1,0:T(8,128)(2,1)} fusion(bf16[1024,512]{1,0:T(8,128)(2,1)S(1)} %multiply_convert_fusion, bf16[1,512,6144]{2,1,0:T(8,128)(2,1)} %param.15), kind=kOutput, calls=%fused_computation.1 | convolution fusion | flops 6448742400 | bytes 19922944 | tf_op jit(solution)/shard_map/dot_general | solution.py:33
  152.0 0.0 reduce-scatter.2.cloned.1.call-update
  152.0 94.8 %reduce-scatter.2.cloned.1.call-done = bf16[64,6144]{1,0:T(8,128)(2,1)} async-done(((bf16[1024,6144]{1,0:T(8,128)(2,1)}), bf16[64,6144]{1,0:T(8,128)(2,1)}) %reduce-scatter.2.cloned.1.call-update) | async-done | bytes 786448 | tf_op jit(solution)/shard_map/reduce_scatter | solution.py:32
  246.8 5.5 %all-to-all-start.1 = ((bf16[8,8,6144]{2,1,0:T(8,128)(2,1)}), bf16[8,8,6144]{2,1,0:T(8,128)(2,1)S(1)}, u32[]{:S(2)}, u32[]{:S(2)}) async-start(bf16[8,8,6144]{2,1,0:T(8,128)(2,1)} %bitcast.24), calls=%async_computation.2 | async-start | bytes 1572864 | tf_op jit(solution)/shard_map/all_to_all | solution.py:39
  252.3 0.1 copy.16
  252.4 0.1 reshape.29
  252.4 0.0 copy-done
  252.5 0.1 copy.15
  252.6 11.9 %all-to-all-done.1 = bf16[8,8,6144]{2,1,0:T(8,128)(2,1)S(1)} async-done(((bf16[8,8,6144]{2,1,0:T(8,128)(2,1)}), bf16[8,8,6144]{2,1,0:T(8,128)(2,1)S(1)}, u32[]{:S(2)}, u32[]{:S(2)}) %all-to-all-start.1) | async-done | bytes 786464 | tf_op jit(solution)/shard_map/all_to_all | solution.py:39
  264.4 0.8 gather_fusion
  265.2 0.5 reshape.37
  265.7 1.7 multiply_reduce_fusion
  (7 shorter events, 0.0 us)
Async XLA Ops:
  6.5 112.6 %all-gather.2.cloned.1.call-start = ((), (), s32[]{:S(2)}) async-start(), calls=%async_computation.3 | async-start | bytes 13369344 | tf_op jit(solution)/shard_map/all_gather | solution.py:27
  28.5 218.3 %reduce-scatter.2.cloned.1.call-start = ((), (), s32[]{:S(2)}) async-start(), calls=%async_computation.4 | async-start | bytes 13369344 | tf_op jit(solution)/shard_map/reduce_scatter | solution.py:32
  119.1 11.6 %copy-start.1 = (bf16[1024,6144]{1,0:T(8,128)(2,1)S(1)}, bf16[1024,6144]{1,0:T(8,128)(2,1)}, u32[]{:S(2)}) copy-start(bf16[1024,6144]{1,0:T(8,128)(2,1)} %all-gather.2.cloned.1.call-done) | copy-start | bytes 37748740
  152.0 100.4 %copy-start = (f32[16,2]{0,1:T(2,128)S(1)}, f32[16,2]{0,1:T(2,128)}, u32[]{:S(2)}) copy-start(f32[16,2]{0,1:T(2,128)} %param.12) | copy-start | bytes 388
  246.8 17.6 %all-to-all-start.1 = ((bf16[8,8,6144]{2,1,0:T(8,128)(2,1)}), bf16[8,8,6144]{2,1,0:T(8,128)(2,1)S(1)}, u32[]{:S(2)}, u32[]{:S(2)}) async-start(bf16[8,8,6144]{2,1,0:T(8,128)(2,1)} %bitcast.24), calls=%async_computation.2 | async-start | bytes 1572864 | tf_op jit(solution)/shard_map/all_to_all | solution.py:39
Sparse Core Ops, SparseCore 0:
  28.6 90.4 all-gather.1
  152.2 94.6 reduce-scatter.1
where the time goes:
time: 275 us; the launch traced here: 274 us
  waiting for transfers between devices  197 us (72%)
  matrix products  34.2 us (12%)
  blocking collectives  18 us (7%)
  between operations  13.5 us (5%)
  starting transfers between devices  5.5 us (2%)
  other arithmetic  4.34 us (2%)
    reduce_scatter x1, waiting for transfers between devices, local(): lax.psum_scatter(jnp.dot(piece, down_local, preferred_element_type=jnp.fl...  94.8 us
    all_gather x1, waiting for transfers between devices, local(): lax.all_gather(arrived.reshape(experts * CAP, features), 'mp', axis=0, ti...  90.6 us
    all_to_all x1, blocking collectives, local(): lax.all_to_all(outgoing, 'expert', split_axis=0, concat_axis=0, tiled=True)  18 us
    dot_general x1, matrix products, local(): jnp.dot(piece, down_local, preferred_element_type=jnp.float32)  12.4 us
    all_to_all x1, waiting for transfers between devices, local(): lax.all_to_all(results, 'expert', split_axis=0, concat_axis=0, tiled=True)  11.9 us
    dot_general x1, matrix products, local(): up_proj = jnp.dot(piece, up_local, preferred_element_type=jnp.float32)  11.6 us
    dot_general x1, matrix products, local(): gate_proj = jnp.dot(piece, gate_local, preferred_element_type=jnp.float32)  8.94 us
  transfers between devices with their start and end apart: 3, of which 3 were waited for; matrix products, arithmetic and copies ran while one was open for 0% of the time, Pallas kernels for 0%

commit v1 on v0

--- a/solution.py
+++ b/solution.py
@@ -24,7 +24,12 @@
     up_local = w_up[0]
     down_local = w_down[0]
     arrived = lax.all_to_all(outgoing, "expert", split_axis=0, concat_axis=0, tiled=True)
-    piece = lax.all_gather(arrived.reshape(experts * CAP, features), "mp", axis=0, tiled=True)
+    piece = jnp.concatenate(
+        lax.all_to_all(
+            jnp.stack([arrived.reshape(experts * CAP, features)] * lax.axis_size("mp")), "mp", 0, 0
+        ),
+        axis=0,
+    )
     gate_proj = jnp.dot(piece, gate_local, preferred_element_type=jnp.float32)
     up_proj = jnp.dot(piece, up_local, preferred_element_type=jnp.float32)
     hidden = (jax.nn.silu(gate_proj) * up_proj).astype(jnp.bfloat16)

time: 275 us -> 331 us (1.20)
  blocking collectives: 18 us -> 165 us
  waiting for transfers between devices: 197 us -> 104 us
  local copies, waits for them, and re-layouts: 1.54 us -> 7.67 us
  matrix products: 34.2 us -> 30 us
    all_to_all x0 -> x1, blocking collectives: none -> 147 us  [local(): lax.all_to_all(jnp.stack([arrived.reshape(experts * CAP, features)] * lax...]
    all_gather x1 -> x0, waiting for transfers between devices: 90.6 us -> none  [local(): lax.all_gather(arrived.reshape(experts * CAP, features), 'mp', axis=0, ti...]
    another operation x0 -> x1, local copies, waits for them, and re-layouts: none -> 6.12 us  [local(): jnp.stack([arrived.reshape(experts * CAP, features)] * lax.axis_size('mp'))]
    dot_general x1, matrix products: 11.6 us -> 7.99 us  [local(): up_proj = jnp.dot(piece, up_local, preferred_element_type=jnp.float32)]
  transfers between devices with their start and end apart: 3 -> 2, of which waited for: 3 -> 2; matrix products, arithmetic and copies ran while one was open for 0% -> 0% of each run, Pallas kernels for 0% -> 0%
where the time goes in v1:
time: 331 us; the launch traced here: 330 us
  blocking collectives  165 us (50%)
  waiting for transfers between devices  104 us (31%)
  matrix products  30 us (9%)
  between operations  13.5 us (4%)
  local copies, waits for them, and re-layouts  7.67 us (2%)
  starting transfers between devices  5.46 us (2%)
  other arithmetic  4.34 us (1%)
    all_to_all x1, blocking collectives, local(): lax.all_to_all(jnp.stack([arrived.reshape(experts * CAP, features)] * lax...  147 us
    reduce_scatter x1, waiting for transfers between devices, local(): lax.psum_scatter(jnp.dot(piece, down_local, preferred_element_type=jnp.fl...  92 us
    all_to_all x1, blocking collectives, local(): lax.all_to_all(outgoing, 'expert', split_axis=0, concat_axis=0, tiled=True)  17.9 us
    dot_general x1, matrix products, local(): jnp.dot(piece, down_local, preferred_element_type=jnp.float32)  12.4 us
    all_to_all x1, waiting for transfers between devices, local(): lax.all_to_all(results, 'expert', split_axis=0, concat_axis=0, tiled=True)  11.9 us
    dot_general x1, matrix products, local(): gate_proj = jnp.dot(piece, gate_local, preferred_element_type=jnp.float32)  8.36 us
    dot_general x1, matrix products, local(): up_proj = jnp.dot(piece, up_local, preferred_element_type=jnp.float32)  7.99 us
  transfers between devices with their start and end apart: 2, of which 2 were waited for; matrix products, arithmetic and copies ran while one was open for 0% of the time, Pallas kernels for 0%

profile of v1, /device:TPU:1, one launch (start us, length us, event | category | flops | bytes accessed | tf_op | source)
XLA Modules:
  0.0 330.2 jit_solution(12669722394944075678)
XLA Ops:
  6.5 0.0 reduce-scatter.2.cloned.1.call-start
  6.5 0.7 compare_select_fusion
  7.2 0.1 fusion.14
  7.3 0.7 convert_element_type.26
  8.0 1.1 fusion.8
  9.1 1.3 fusion
  10.5 17.9 %all_to_all.15 = bf16[8,8,6144]{2,1,0:T(8,128)(2,1)S(1)} all-to-all(bf16[8,8,6144]{2,1,0:T(8,128)(2,1)S(1)} %fusion), channel_id=1, replica_groups=mesh['expert'=8,'mp'=16] {'expert'}, dimensions={0} | all-to-all | bytes 1572864 | tf_op jit(solution)/shard_map/all_to_all | solution.py:26
  28.4 6.1 %stack.3 = bf16[16,64,6144]{2,1,0:T(8,128)(2,1)} broadcast(bf16[64,6144]{1,0:T(8,128)(2,1)S(1)} %bitcast.26), dimensions={1,2} | broadcast | bytes 13369344 | tf_op jit(solution)/shard_map/stack | solution.py:29
  34.5 147.4 %all_to_all.16 = bf16[16,64,6144]{2,1,0:T(8,128)(2,1)S(1)} all-to-all(bf16[16,64,6144]{2,1,0:T(8,128)(2,1)} %stack.3), channel_id=1, replica_groups=mesh['expert'=8,'mp'=16] {'mp'}, dimensions={0} | all-to-all | bytes 25165824 | tf_op jit(solution)/shard_map/all_to_all | solution.py:28
  181.9 0.0 slice-done
  181.9 8.0 %fusion.2 = f32[1024,512]{1,0:T(8,128)} fusion(bf16[1024,6144]{1,0:T(8,128)(2,1)S(1)} %bitcast.24, bf16[1,6144,512]{2,1,0:T(8,128)(2,1)S(1)} %bitcast.29), kind=kOutput, calls=%fused_computation.5 | convolution fusion | flops 6442450944 | bytes 20971520 | tf_op jit(solution)/shard_map/dot_general | solution.py:34
  189.9 0.0 slice-done.3
  189.9 8.4 %multiply_convert_fusion = bf16[1024,512]{1,0:T(8,128)(2,1)S(1)} fusion(f32[1024,512]{1,0:T(8,128)} %fusion.2, bf16[1024,6144]{1,0:T(8,128)(2,1)S(1)} %bitcast.25, bf16[1,6144,512]{2,1,0:T(8,128)(2,1)S(1)} %bitcast.31), kind=kOutput, calls=%fused_computation.9 | convolution fusion | flops 6445596672 | bytes 22020096 | tf_op jit(solution)/shard_map/dot_general | solution.py:33
  198.3 12.4 %convolution_convert_fusion = bf16[1024,6144]{1,0:T(8,128)(2,1)} fusion(bf16[1024,512]{1,0:T(8,128)(2,1)S(1)} %multiply_convert_fusion, bf16[1,512,6144]{2,1,0:T(8,128)(2,1)} %param.15), kind=kOutput, calls=%fused_computation.1 | convolution fusion | flops 6448742400 | bytes 19922944 | tf_op jit(solution)/shard_map/dot_general | solution.py:38
  210.6 0.0 reduce-scatter.2.cloned.1.call-update
  210.7 92.0 %reduce-scatter.2.cloned.1.call-done = bf16[64,6144]{1,0:T(8,128)(2,1)} async-done(((bf16[1024,6144]{1,0:T(8,128)(2,1)}), bf16[64,6144]{1,0:T(8,128)(2,1)}) %reduce-scatter.2.cloned.1.call-update) | async-done | bytes 786448 | tf_op jit(solution)/shard_map/reduce_scatter | solution.py:37
  302.7 5.5 %all-to-all-start.2 = ((bf16[8,8,6144]{2,1,0:T(8,128)(2,1)}), bf16[8,8,6144]{2,1,0:T(8,128)(2,1)S(1)}, u32[]{:S(2)}, u32[]{:S(2)}) async-start(bf16[8,8,6144]{2,1,0:T(8,128)(2,1)} %bitcast.27), calls=%async_computation.3 | async-start | bytes 1572864 | tf_op jit(solution)/shard_map/all_to_all | solution.py:44
  308.1 0.1 copy.16
  308.2 0.1 reshape.31
  308.4 0.1 copy.15
  308.4 11.9 %all-to-all-done.2 = bf16[8,8,6144]{2,1,0:T(8,128)(2,1)S(1)} async-done(((bf16[8,8,6144]{2,1,0:T(8,128)(2,1)}), bf16[8,8,6144]{2,1,0:T(8,128)(2,1)S(1)}, u32[]{:S(2)}, u32[]{:S(2)}) %all-to-all-start.2) | async-done | bytes 786464 | tf_op jit(solution)/shard_map/all_to_all | solution.py:44
  320.3 0.8 gather_fusion
  321.1 0.5 reshape.39
  321.6 1.7 multiply_reduce_fusion
  (14 shorter events, 0.0 us)
Async XLA Ops:
  6.5 296.2 %reduce-scatter.2.cloned.1.call-start = ((), (), s32[]{:S(2)}) async-start(), calls=%async_computation.4 | async-start | bytes 13369344 | tf_op jit(solution)/shard_map/reduce_scatter | solution.py:37
  28.4 153.6 %slice-start = ((s8[6291456]{0:T(1024)(128)(4,1)}), s8[2097152]{0:T(1024)(128)(4,1)S(1)}, s32[]{:S(2)}) async-start(s8[6291456]{0:T(1024)(128)(4,1)} %bitcast.28), calls=%async_computation.5 | async-start | bytes 4194304
  34.5 147.4 %slice-start.1 = ((s8[6291456]{0:T(1024)(128)(4,1)}), s8[4194304]{0:T(1024)(128)(4,1)S(1)}, s32[]{:S(2)}) async-start(s8[6291456]{0:T(1024)(128)(4,1)} %bitcast.28), calls=%async_computation.6 | async-start | bytes 8388608
  34.5 155.4 %slice-start.2 = ((s8[6291456]{0:T(1024)(128)(4,1)}), s8[4194304]{0:T(1024)(128)(4,1)S(1)}, s32[]{:S(2)}) async-start(s8[6291456]{0:T(1024)(128)(4,1)} %bitcast.30), calls=%async_computation.7 | async-start | bytes 8388608
  181.9 8.0 %slice-start.3 = ((s8[6291456]{0:T(1024)(128)(4,1)}), s8[2097152]{0:T(1024)(128)(4,1)S(1)}, s32[]{:S(2)}) async-start(s8[6291456]{0:T(1024)(128)(4,1)} %bitcast.30), calls=%async_computation.8 | async-start | bytes 4194304
  210.6 97.7 %copy-start = (f32[16,2]{0,1:T(2,128)S(1)}, f32[16,2]{0,1:T(2,128)}, u32[]{:S(2)}) copy-start(f32[16,2]{0,1:T(2,128)} %param.12) | copy-start | bytes 388
  302.7 17.6 %all-to-all-start.2 = ((bf16[8,8,6144]{2,1,0:T(8,128)(2,1)}), bf16[8,8,6144]{2,1,0:T(8,128)(2,1)S(1)}, u32[]{:S(2)}, u32[]{:S(2)}) async-start(bf16[8,8,6144]{2,1,0:T(8,128)(2,1)} %bitcast.27), calls=%async_computation.3 | async-start | bytes 1572864 | tf_op jit(solution)/shard_map/all_to_all | solution.py:44
Sparse Core Ops, SparseCore 0:
  210.8 91.8 reduce-scatter.1
